TPU v7x, 32 devices: a whole 2x2x4 slice. The times are simulated.
32 devices in a mesh: seq: 8 (over y, x, core), head: 4 (over z).
Axes of the slice: x: 2, y: 2, z: 4, core: 2. Of those that a mesh axis runs over, the one named last changes fastest.
Arguments:
- queries: bfloat16 [4096, 4096], P('seq', 'head'), may hold values from -7 to 7
- keys: bfloat16 [32768, 1024], P('seq', 'head'), may hold values from -4 to 4
- values: bfloat16 [32768, 1024], P('seq', 'head'), may hold values from -5 to 5
- out_grad: bfloat16 [4096, 4096], P('seq', 'head'), may hold values from -6 to 6
- out_weight: bfloat16 [4096, 4096], P('head'), may hold values from -0.09375 to 0.09375
- selected: int32 [8, 6], replicated, may hold values from 0 to 63, as said below
Outputs:
- query_grad: bfloat16 [4096, 4096], P('seq', 'head')
- key_grad: bfloat16 [32768, 1024], P('seq', 'head')
- value_grad: bfloat16 [32768, 1024], P('seq', 'head')
Inputs may be any that keep to these rules, and one draw needn't show every extreme that they name: `selected`: row i lists first the block i * 8 + 7, then 5 further distinct blocks of lower number; among them at most one lies in the run of 8 blocks j * 8 to j * 8 + 7 of any j other than i, and every row i >= 1 lists exactly one block of the run of j = 0.
All inputs are finite; a program needn't handle non-finite values.
Results may differ from a plain program's by a relative error of at most 0.0095.
Values may be sent and summed in bfloat16 or wider, within the bound.
No kernel may reach another device: no remote copies, remote signals or barrier semaphores. Data moves between devices by JAX's collectives and lax.ppermute only.
A program may use at most 128 MiB of HBM per device.

v0:
```python
import jax
import jax.numpy as jnp
from jax import lax
from jax.sharding import PartitionSpec as P

HEAD_DIM = 128
BLOCK = 512
TOPK = 6


def score_tile(query_head, key_head, factor, visible):
    scores = (
        lax.dot_general(
            query_head, key_head, (((1,), (1,)), ((), ())), preferred_element_type=jnp.float32
        )
        * factor
    )
    return jnp.where(visible, scores, -jnp.inf)


def shards(queries, keys, values, out_grad, out_weight, selected):
    factor = HEAD_DIM ** (-0.5)
    kv_cols = keys.shape[1]
    kv_local = kv_cols // HEAD_DIM
    q_local = queries.shape[1] // HEAD_DIM
    group_size = q_local // kv_local
    blocks_here = keys.shape[0] // BLOCK
    length = TOPK * BLOCK
    devices = lax.axis_size("seq")
    position = lax.axis_index("seq")
    grad_output = lax.dot_general(
        lax.all_gather(out_grad, "head", axis=1, tiled=True),
        out_weight,
        (((1,), (1,)), ((), ())),
        preferred_element_type=jnp.float32,
    ).astype(jnp.bfloat16)
    senders = jnp.arange(devices, dtype=jnp.int32)[:, None]
    my_picks = lax.dynamic_index_in_dim(selected, position, 0, keepdims=False)
    my_owner = my_picks // blocks_here
    my_inner = my_picks % blocks_here
    is_remote = my_owner != position
    key_tiles = keys.reshape(blocks_here, BLOCK, kv_cols)
    value_tiles = values.reshape(blocks_here, BLOCK, kv_cols)
    column = lax.broadcasted_iota(jnp.int32, (BLOCK, length), 1)
    rowpos = lax.broadcasted_iota(jnp.int32, (BLOCK, length), 0)
    visible = (column >= BLOCK) | (column <= rowpos)
    owners = selected // blocks_here
    inners = selected % blocks_here
    wanted = (owners == position) & (senders != position)
    send_index = jnp.sum(jnp.where(wanted, inners, 0), axis=1)
    send_keys = jnp.take(key_tiles, send_index, axis=0)
    send_values = jnp.take(value_tiles, send_index, axis=0)
    arrived_keys, arrived_values = (
        lax.all_to_all(send_keys, "seq", split_axis=0, concat_axis=0, tiled=True),
        lax.all_to_all(send_values, "seq", split_axis=0, concat_axis=0, tiled=True),
    )

    def assemble(arrived, local_tiles):
        remote_rows = jnp.take(arrived, my_owner, axis=0)
        local_rows = jnp.take(local_tiles, my_inner, axis=0)
        return jnp.where(is_remote[:, None, None], remote_rows, local_rows).reshape(length, kv_cols)

    slot_keys = assemble(arrived_keys, key_tiles)
    slot_values = assemble(arrived_values, value_tiles)

    def one_head(head_index, running):
        query_acc, key_acc, value_acc = running
        kv_index = head_index // group_size
        query_head = lax.dynamic_slice_in_dim(queries, head_index * HEAD_DIM, HEAD_DIM, 1)
        grad_head = lax.dynamic_slice_in_dim(grad_output, head_index * HEAD_DIM, HEAD_DIM, 1)
        key_head = lax.dynamic_slice_in_dim(slot_keys, kv_index * HEAD_DIM, HEAD_DIM, 1)
        value_head = lax.dynamic_slice_in_dim(slot_values, kv_index * HEAD_DIM, HEAD_DIM, 1)
        scores = score_tile(query_head, key_head, factor, visible)
        row_max = jnp.max(scores, axis=1, keepdims=True)
        shifted = jnp.exp(scores - row_max)
        weights = shifted / jnp.sum(shifted, axis=1, keepdims=True)
        weights_low = weights.astype(jnp.bfloat16)
        attended = jnp.dot(weights_low, value_head, preferred_element_type=jnp.float32)
        row_dot = jnp.sum(grad_head.astype(jnp.float32) * attended, axis=1, keepdims=True)
        value_part = lax.dot_general(
            weights_low, grad_head, (((0,), (0,)), ((), ())), preferred_element_type=jnp.float32
        )
        grad_weights = lax.dot_general(
            grad_head, value_head, (((1,), (1,)), ((), ())), preferred_element_type=jnp.float32
        )
        grad_low = (weights * (grad_weights - row_dot)).astype(jnp.bfloat16)
        query_part = jnp.dot(grad_low, key_head, preferred_element_type=jnp.float32) * factor
        key_part = (
            lax.dot_general(
                grad_low, query_head, (((0,), (0,)), ((), ())), preferred_element_type=jnp.float32
            )
            * factor
        )
        query_acc = lax.dynamic_update_slice_in_dim(query_acc, query_part, head_index * HEAD_DIM, 1)
        old_key = lax.dynamic_slice_in_dim(key_acc, kv_index * HEAD_DIM, HEAD_DIM, 1)
        key_acc = lax.dynamic_update_slice_in_dim(
            key_acc, old_key + key_part, kv_index * HEAD_DIM, 1
        )
        old_value = lax.dynamic_slice_in_dim(value_acc, kv_index * HEAD_DIM, HEAD_DIM, 1)
        value_acc = lax.dynamic_update_slice_in_dim(
            value_acc, old_value + value_part, kv_index * HEAD_DIM, 1
        )
        return (query_acc, key_acc, value_acc)

    initial_acc = (
        jnp.zeros((BLOCK, q_local * HEAD_DIM), jnp.float32),
        jnp.zeros((length, kv_cols), jnp.float32),
        jnp.zeros((length, kv_cols), jnp.float32),
    )
    query_acc, key_acc, value_acc = lax.fori_loop(0, q_local, one_head, initial_acc)
    query_grad = query_acc.astype(jnp.bfloat16)
    key_low = key_acc.astype(jnp.bfloat16).reshape(TOPK, BLOCK, kv_cols)
    value_low = value_acc.astype(jnp.bfloat16).reshape(TOPK, BLOCK, kv_cols)
    owners_all = selected // blocks_here
    wanted_all = (owners_all == position) & (senders != position)
    index_all = jnp.sum(jnp.where(wanted_all, selected % blocks_here, 0), axis=1)
    has_pick = jnp.any(wanted_all, axis=1)
    route_back = ((my_owner[None, :] == senders) & is_remote[None, :]).astype(jnp.bfloat16)
    back_keys = jnp.einsum(
        "er,rbc->ebc", route_back, key_low, preferred_element_type=jnp.float32
    ).astype(jnp.bfloat16)
    back_values = jnp.einsum(
        "er,rbc->ebc", route_back, value_low, preferred_element_type=jnp.float32
    ).astype(jnp.bfloat16)
    arrived_kgrad, arrived_vgrad = (
        lax.all_to_all(back_keys, "seq", split_axis=0, concat_axis=0, tiled=True),
        lax.all_to_all(back_values, "seq", split_axis=0, concat_axis=0, tiled=True),
    )
    tile_ids = jnp.arange(blocks_here, dtype=jnp.int32)[:, None]
    from_peers = ((index_all[None, :] == tile_ids) & has_pick[None, :]).astype(jnp.bfloat16)
    from_self = ((my_inner[None, :] == tile_ids) & jnp.logical_not(is_remote)[None, :]).astype(
        jnp.bfloat16
    )
    key_total = jnp.einsum(
        "je,ebc->jbc", from_peers, arrived_kgrad, preferred_element_type=jnp.float32
    ) + jnp.einsum("jr,rbc->jbc", from_self, key_low, preferred_element_type=jnp.float32)
    value_total = jnp.einsum(
        "je,ebc->jbc", from_peers, arrived_vgrad, preferred_element_type=jnp.float32
    ) + jnp.einsum("jr,rbc->jbc", from_self, value_low, preferred_element_type=jnp.float32)
    key_grad = key_total.astype(jnp.bfloat16).reshape(blocks_here * BLOCK, kv_cols)
    value_grad = value_total.astype(jnp.bfloat16).reshape(blocks_here * BLOCK, kv_cols)
    return (query_grad, key_grad, value_grad)


def solution(mesh):
    in_specs = (
        P("seq", "head"),
        P("seq", "head"),
        P("seq", "head"),
        P("seq", "head"),
        P("head", None),
        P(),
    )
    out_specs = (P("seq", "head"), P("seq", "head"), P("seq", "head"))
    return jax.shard_map(shards, mesh=mesh, in_specs=in_specs, out_specs=out_specs, check_vma=False)
```

profile of v0, /device:TPU:0, one launch (start us, length us, event | category | flops | bytes accessed | tf_op | source)
XLA Modules:
  0.0 366.2 jit_solution(18069912691345344136)
XLA Ops:
  9.6 3.6 gather_fusion
  13.2 2.0 gather_fusion.3
  15.2 4.0 %broadcast_select_fusion = (bf16[8,512,256]{2,1,0:T(8,128)(2,1)S(1)}, bf16[8,512,256]{2,1,0:T(8,128)(2,1)}) fusion(bf16[8,512,256]{2,1,0:T(8,128)(2,1)} %gather_fusion.3, pred[8]{0:T(512)(128)(4,1)S(1)} %compare_and_fusion.2, bf16[8,512,256]{2,1,0:T(8,128)(2,1)} %gather_fusion), kind=kLoop, calls=%fused_computation.50 | loop fusion | flops 2097152 | bytes 8388616 | tf_op jit(solution)/shard_map/jit(_take)/select_n | solution.py:52
  19.2 31.7 %all_to_all.20 = bf16[8,512,256]{2,1,0:T(8,128)(2,1)} all-to-all(bf16[8,512,256]{2,1,0:T(8,128)(2,1)S(1)} %get-tuple-element.310), channel_id=1, replica_groups=mesh['seq'=8,'head'=4] {'seq'}, dimensions={0} | all-to-all | bytes 4194304 | tf_op jit(solution)/shard_map/all_to_all | solution.py:55
  50.9 4.3 %all-to-all-start = ((bf16[8,512,256]{2,1,0:T(8,128)(2,1)}), bf16[8,512,256]{2,1,0:T(8,128)(2,1)}, u32[]{:S(2)}, u32[]{:S(2)}) async-start(bf16[8,512,256]{2,1,0:T(8,128)(2,1)} %get-tuple-element.311), calls=%async_computation | async-start | bytes 4194304 | tf_op jit(solution)/shard_map/all_to_all | solution.py:54
  56.0 1.8 gather_fusion.5
  57.8 3.6 gather_fusion.2
  61.5 1.8 gather_fusion.4
  63.4 18.5 %all-to-all-done = bf16[8,512,256]{2,1,0:T(8,128)(2,1)} async-done(((bf16[8,512,256]{2,1,0:T(8,128)(2,1)}), bf16[8,512,256]{2,1,0:T(8,128)(2,1)}, u32[]{:S(2)}, u32[]{:S(2)}) %all-to-all-start) | async-done | bytes 2097184 | tf_op jit(solution)/shard_map/all_to_all | solution.py:54
  81.8 3.4 gather_fusion.1
  85.3 4.5 %select_select_fusion = (bf16[6,512,256]{2,1,0:T(8,128)(2,1)S(1)}, bf16[6,512,256]{2,1,0:T(8,128)(2,1)}) fusion(bf16[6,512,256]{2,1,0:T(8,128)(2,1)} %gather_fusion.5, bf16[6,512,256]{2,1,0:T(8,128)(2,1)} %gather_fusion.4, pred[6]{0:T(512)(128)(4,1)S(1)} %get-tuple-element.312, pred[6]{0:T(512)(128)(4,1)S(1)} %compare_and_fusion.1, ...), kind=kLoop, calls=%fused_computation.54 | loop fusion | flops 4718592 | bytes 9437202 | tf_op jit(solution)/shard_map/jit(_where)/select_n | solution.py:61
  89.8 3.2 all-gather.2.cloned.1.call-done
  93.1 10.1 %convolution_convert_fusion = bf16[512,1024]{1,0:T(8,128)(2,1)} fusion(bf16[512,4096]{1,0:T(8,128)(2,1)} %all-gather.2.cloned.1.call-done, bf16[1024,4096]{1,0:T(8,128)(2,1)} %param.16), kind=kOutput, calls=%fused_computation.56 | convolution fusion | flops 4295491584 | bytes 13631488 | tf_op jit(solution)/shard_map/dot_general | solution.py:31
  103.2 1.9 broadcast.159
  105.1 1.9 broadcast.159.clone
  107.1 179.1 %while.20 = (s32[]{:T(128)}, bf16[512,1024]{1,0:T(8,128)(2,1)S(1)}, f32[3072,256]{1,0:T(8,128)}, f32[3072,256]{1,0:T(8,128)}, bf16[512,1024]{1,0:T(8,128)(2,1)},...) while((s32[]{:T(128)}, bf16[512,1024]{1,0:T(8,128)(2,1)S(1)}, ...), condition=%wide.region_5.8_spmd.clone, body=%wide.region_1.7_spmd.clone.sunk | while | flops 2439379456 | bytes 120997328 | solution.py:110
  107.3 2.4 fusion.112
  110.7 3.9 %fusion.114 = f32[512,3072]{1,0:T(8,128)} fusion(f32[512,3072]{1,0:T(8,128)S(1)} %get-tuple-element.371, f32[512]{0:T(512)S(1)} %fusion.113, f32[512]{0:T(512)S(1)} %get-tuple-element.372), kind=kLoop, calls=%fused_computation.12.clone.1 | loop fusion | flops 3145728 | bytes 12587008 | tf_op jit(solution)/shard_map/while/body/eval_jaxpr/div | solution.py:76
  115.7 4.1 %fusion.115 = f32[512]{0:T(512)S(1)} fusion(f32[512,3072]{1,0:T(8,128)} %fusion.114, bf16[3072,256]{1,0:T(8,128)(2,1)S(1)} %get-tuple-element.414, s32[]{:T(128)S(6)} %select_n.198, bf16[512,128]{0,1:T(8,128)(2,1)S(1)} %copy.46), kind=kOutput, calls=%fused_computation.25.clone.1 | convolution fusion | flops 404422144 | bytes 7211012 | tf_op jit(solution)/shard_map/while/body/eval_jaxpr/dot_general | solution.py:78
  122.1 2.2 fusion.117
  126.1 3.7 fusion.118
  129.7 2.4 fusion.112
  133.1 3.9 %fusion.114 = f32[512,3072]{1,0:T(8,128)} fusion(f32[512,3072]{1,0:T(8,128)S(1)} %get-tuple-element.371, f32[512]{0:T(512)S(1)} %fusion.113, f32[512]{0:T(512)S(1)} %get-tuple-element.372), kind=kLoop, calls=%fused_computation.12.clone.1 | loop fusion | flops 3145728 | bytes 12587008 | tf_op jit(solution)/shard_map/while/body/eval_jaxpr/div | solution.py:76
  138.0 4.1 %fusion.115 = f32[512]{0:T(512)S(1)} fusion(f32[512,3072]{1,0:T(8,128)} %fusion.114, bf16[3072,256]{1,0:T(8,128)(2,1)S(1)} %get-tuple-element.414, s32[]{:T(128)S(6)} %select_n.198, bf16[512,128]{0,1:T(8,128)(2,1)S(1)} %copy.46), kind=kOutput, calls=%fused_computation.25.clone.1 | convolution fusion | flops 404422144 | bytes 7211012 | tf_op jit(solution)/shard_map/while/body/eval_jaxpr/dot_general | solution.py:78
  144.5 2.2 fusion.117
  148.4 3.7 fusion.118
  152.1 2.4 fusion.112
  155.4 3.9 %fusion.114 = f32[512,3072]{1,0:T(8,128)} fusion(f32[512,3072]{1,0:T(8,128)S(1)} %get-tuple-element.371, f32[512]{0:T(512)S(1)} %fusion.113, f32[512]{0:T(512)S(1)} %get-tuple-element.372), kind=kLoop, calls=%fused_computation.12.clone.1 | loop fusion | flops 3145728 | bytes 12587008 | tf_op jit(solution)/shard_map/while/body/eval_jaxpr/div | solution.py:76
  160.4 4.1 %fusion.115 = f32[512]{0:T(512)S(1)} fusion(f32[512,3072]{1,0:T(8,128)} %fusion.114, bf16[3072,256]{1,0:T(8,128)(2,1)S(1)} %get-tuple-element.414, s32[]{:T(128)S(6)} %select_n.198, bf16[512,128]{0,1:T(8,128)(2,1)S(1)} %copy.46), kind=kOutput, calls=%fused_computation.25.clone.1 | convolution fusion | flops 404422144 | bytes 7211012 | tf_op jit(solution)/shard_map/while/body/eval_jaxpr/dot_general | solution.py:78
  166.9 2.2 fusion.117
  170.8 3.7 fusion.118
  174.5 2.4 fusion.112
  177.8 3.9 %fusion.114 = f32[512,3072]{1,0:T(8,128)} fusion(f32[512,3072]{1,0:T(8,128)S(1)} %get-tuple-element.371, f32[512]{0:T(512)S(1)} %fusion.113, f32[512]{0:T(512)S(1)} %get-tuple-element.372), kind=kLoop, calls=%fused_computation.12.clone.1 | loop fusion | flops 3145728 | bytes 12587008 | tf_op jit(solution)/shard_map/while/body/eval_jaxpr/div | solution.py:76
  182.8 4.1 %fusion.115 = f32[512]{0:T(512)S(1)} fusion(f32[512,3072]{1,0:T(8,128)} %fusion.114, bf16[3072,256]{1,0:T(8,128)(2,1)S(1)} %get-tuple-element.414, s32[]{:T(128)S(6)} %select_n.198, bf16[512,128]{0,1:T(8,128)(2,1)S(1)} %copy.46), kind=kOutput, calls=%fused_computation.25.clone.1 | convolution fusion | flops 404422144 | bytes 7211012 | tf_op jit(solution)/shard_map/while/body/eval_jaxpr/dot_general | solution.py:78
  189.3 2.2 fusion.117
  193.2 3.7 fusion.118
  196.8 2.4 fusion.112
  200.2 3.9 %fusion.114 = f32[512,3072]{1,0:T(8,128)} fusion(f32[512,3072]{1,0:T(8,128)S(1)} %get-tuple-element.371, f32[512]{0:T(512)S(1)} %fusion.113, f32[512]{0:T(512)S(1)} %get-tuple-element.372), kind=kLoop, calls=%fused_computation.12.clone.1 | loop fusion | flops 3145728 | bytes 12587008 | tf_op jit(solution)/shard_map/while/body/eval_jaxpr/div | solution.py:76
  205.2 4.1 %fusion.115 = f32[512]{0:T(512)S(1)} fusion(f32[512,3072]{1,0:T(8,128)} %fusion.114, bf16[3072,256]{1,0:T(8,128)(2,1)S(1)} %get-tuple-element.414, s32[]{:T(128)S(6)} %select_n.198, bf16[512,128]{0,1:T(8,128)(2,1)S(1)} %copy.46), kind=kOutput, calls=%fused_computation.25.clone.1 | convolution fusion | flops 404422144 | bytes 7211012 | tf_op jit(solution)/shard_map/while/body/eval_jaxpr/dot_general | solution.py:78
  211.6 2.2 fusion.117
  215.5 3.6 fusion.118
  219.2 2.4 fusion.112
  222.5 3.9 %fusion.114 = f32[512,3072]{1,0:T(8,128)} fusion(f32[512,3072]{1,0:T(8,128)S(1)} %get-tuple-element.371, f32[512]{0:T(512)S(1)} %fusion.113, f32[512]{0:T(512)S(1)} %get-tuple-element.372), kind=kLoop, calls=%fused_computation.12.clone.1 | loop fusion | flops 3145728 | bytes 12587008 | tf_op jit(solution)/shard_map/while/body/eval_jaxpr/div | solution.py:76
  227.5 4.1 %fusion.115 = f32[512]{0:T(512)S(1)} fusion(f32[512,3072]{1,0:T(8,128)} %fusion.114, bf16[3072,256]{1,0:T(8,128)(2,1)S(1)} %get-tuple-element.414, s32[]{:T(128)S(6)} %select_n.198, bf16[512,128]{0,1:T(8,128)(2,1)S(1)} %copy.46), kind=kOutput, calls=%fused_computation.25.clone.1 | convolution fusion | flops 404422144 | bytes 7211012 | tf_op jit(solution)/shard_map/while/body/eval_jaxpr/dot_general | solution.py:78
  234.0 2.2 fusion.117
  237.9 3.6 fusion.118
  241.5 2.4 fusion.112
  244.9 3.9 %fusion.114 = f32[512,3072]{1,0:T(8,128)} fusion(f32[512,3072]{1,0:T(8,128)S(1)} %get-tuple-element.371, f32[512]{0:T(512)S(1)} %fusion.113, f32[512]{0:T(512)S(1)} %get-tuple-element.372), kind=kLoop, calls=%fused_computation.12.clone.1 | loop fusion | flops 3145728 | bytes 12587008 | tf_op jit(solution)/shard_map/while/body/eval_jaxpr/div | solution.py:76
  249.8 4.1 %fusion.115 = f32[512]{0:T(512)S(1)} fusion(f32[512,3072]{1,0:T(8,128)} %fusion.114, bf16[3072,256]{1,0:T(8,128)(2,1)S(1)} %get-tuple-element.414, s32[]{:T(128)S(6)} %select_n.198, bf16[512,128]{0,1:T(8,128)(2,1)S(1)} %copy.46), kind=kOutput, calls=%fused_computation.25.clone.1 | convolution fusion | flops 404422144 | bytes 7211012 | tf_op jit(solution)/shard_map/while/body/eval_jaxpr/dot_general | solution.py:78
  256.3 2.2 fusion.117
  260.2 3.6 fusion.118
  263.9 2.4 fusion.112
  267.2 3.9 %fusion.114 = f32[512,3072]{1,0:T(8,128)} fusion(f32[512,3072]{1,0:T(8,128)S(1)} %get-tuple-element.371, f32[512]{0:T(512)S(1)} %fusion.113, f32[512]{0:T(512)S(1)} %get-tuple-element.372), kind=kLoop, calls=%fused_computation.12.clone.1 | loop fusion | flops 3145728 | bytes 12587008 | tf_op jit(solution)/shard_map/while/body/eval_jaxpr/div | solution.py:76
  272.2 4.1 %fusion.115 = f32[512]{0:T(512)S(1)} fusion(f32[512,3072]{1,0:T(8,128)} %fusion.114, bf16[3072,256]{1,0:T(8,128)(2,1)S(1)} %get-tuple-element.414, s32[]{:T(128)S(6)} %select_n.198, bf16[512,128]{0,1:T(8,128)(2,1)S(1)} %copy.46), kind=kOutput, calls=%fused_computation.25.clone.1 | convolution fusion | flops 404422144 | bytes 7211012 | tf_op jit(solution)/shard_map/while/body/eval_jaxpr/dot_general | solution.py:78
  278.7 2.2 fusion.117
  282.6 3.6 fusion.118
  286.2 2.4 convert_element_type.62
  291.5 4.3 %all-to-all-start.3 = ((bf16[8,512,256]{2,1,0:T(8,128)(2,1)}), bf16[8,512,256]{2,1,0:T(8,128)(2,1)}, u32[]{:S(2)}, u32[]{:S(2)}) async-start(bf16[8,512,256]{2,1,0:T(8,128)(2,1)} %copy.24), calls=%async_computation.3 | async-start | bytes 4194304 | tf_op jit(solution)/shard_map/all_to_all | solution.py:127
  295.9 2.0 convert_element_type.59
  300.8 21.7 %all-to-all-done.3 = bf16[8,512,256]{2,1,0:T(8,128)(2,1)} async-done(((bf16[8,512,256]{2,1,0:T(8,128)(2,1)}), bf16[8,512,256]{2,1,0:T(8,128)(2,1)}, u32[]{:S(2)}, u32[]{:S(2)}) %all-to-all-start.3) | async-done | bytes 2097184 | tf_op jit(solution)/shard_map/all_to_all | solution.py:127
  322.5 4.6 %all-to-all-start.2 = ((bf16[8,512,256]{2,1,0:T(8,128)(2,1)}), bf16[8,512,256]{2,1,0:T(8,128)(2,1)}, u32[]{:S(2)}, u32[]{:S(2)}) async-start(bf16[8,512,256]{2,1,0:T(8,128)(2,1)} %copy.19), calls=%async_computation.2 | async-start | bytes 4194304 | tf_op jit(solution)/shard_map/all_to_all | solution.py:126
  327.1 3.0 fusion.35
  333.0 20.5 %all-to-all-done.2 = bf16[8,512,256]{2,1,0:T(8,128)(2,1)} async-done(((bf16[8,512,256]{2,1,0:T(8,128)(2,1)}), bf16[8,512,256]{2,1,0:T(8,128)(2,1)}, u32[]{:S(2)}, u32[]{:S(2)}) %all-to-all-start.2) | async-done | bytes 2097184 | tf_op jit(solution)/shard_map/all_to_all | solution.py:126
  353.5 3.0 fusion.37
  (146 shorter events, 63.3 us)
Async XLA Ops:
  7.2 6.1 %copy-start = (bf16[4096,256]{1,0:T(8,128)(2,1)S(1)}, bf16[4096,256]{1,0:T(8,128)(2,1)}, u32[]{:S(2)}) copy-start(bf16[4096,256]{1,0:T(8,128)(2,1)} %param.14) | copy-start | bytes 6291460
  7.2 85.9 %all-gather.2.cloned.1.call-start = ((), (), s32[]{:S(2)}) async-start(), calls=%async_computation.4 | async-start | bytes 5242880 | tf_op jit(solution)/shard_map/all_gather | solution.py:32
  50.9 31.0 %all-to-all-start = ((bf16[8,512,256]{2,1,0:T(8,128)(2,1)}), bf16[8,512,256]{2,1,0:T(8,128)(2,1)}, u32[]{:S(2)}, u32[]{:S(2)}) async-start(bf16[8,512,256]{2,1,0:T(8,128)(2,1)} %get-tuple-element.311), calls=%async_computation | async-start | bytes 4194304 | tf_op jit(solution)/shard_map/all_to_all | solution.py:54
  57.8 3.7 %copy-start.10 = (bf16[8,512,256]{2,1,0:T(8,128)(2,1)S(1)}, bf16[8,512,256]{2,1,0:T(8,128)(2,1)}, u32[]{:S(2)}) copy-start(bf16[8,512,256]{2,1,0:T(8,128)(2,1)} %all_to_all.20) | copy-start | bytes 6291460
  115.6 4.6 %copy-start.2 = (f32[512,3072]{1,0:T(8,128)S(1)}, f32[512,3072]{1,0:T(8,128)}, u32[]{:S(2)}) copy-start(f32[512,3072]{1,0:T(8,128)} %fusion.114) | copy-start | bytes 18874372 | tf_op jit(solution)/shard_map/while
  120.2 1.9 copy-start.3
  122.1 2.2 copy-start.9
  124.3 1.7 copy-start.4
  138.0 4.6 %copy-start.2 = (f32[512,3072]{1,0:T(8,128)S(1)}, f32[512,3072]{1,0:T(8,128)}, u32[]{:S(2)}) copy-start(f32[512,3072]{1,0:T(8,128)} %fusion.114) | copy-start | bytes 18874372 | tf_op jit(solution)/shard_map/while
  142.6 1.9 copy-start.3
  144.5 2.2 copy-start.9
  146.7 1.7 copy-start.4
  160.4 4.6 %copy-start.2 = (f32[512,3072]{1,0:T(8,128)S(1)}, f32[512,3072]{1,0:T(8,128)}, u32[]{:S(2)}) copy-start(f32[512,3072]{1,0:T(8,128)} %fusion.114) | copy-start | bytes 18874372 | tf_op jit(solution)/shard_map/while
  165.0 1.9 copy-start.3
  166.9 2.2 copy-start.9
  169.1 1.7 copy-start.4
  182.8 4.6 %copy-start.2 = (f32[512,3072]{1,0:T(8,128)S(1)}, f32[512,3072]{1,0:T(8,128)}, u32[]{:S(2)}) copy-start(f32[512,3072]{1,0:T(8,128)} %fusion.114) | copy-start | bytes 18874372 | tf_op jit(solution)/shard_map/while
  187.4 1.9 copy-start.3
  189.3 2.2 copy-start.9
  191.5 1.7 copy-start.4
  205.1 4.6 %copy-start.2 = (f32[512,3072]{1,0:T(8,128)S(1)}, f32[512,3072]{1,0:T(8,128)}, u32[]{:S(2)}) copy-start(f32[512,3072]{1,0:T(8,128)} %fusion.114) | copy-start | bytes 18874372 | tf_op jit(solution)/shard_map/while
  209.7 1.9 copy-start.3
  211.6 2.2 copy-start.9
  213.8 1.7 copy-start.4
  227.5 4.6 %copy-start.2 = (f32[512,3072]{1,0:T(8,128)S(1)}, f32[512,3072]{1,0:T(8,128)}, u32[]{:S(2)}) copy-start(f32[512,3072]{1,0:T(8,128)} %fusion.114) | copy-start | bytes 18874372 | tf_op jit(solution)/shard_map/while
  232.1 1.9 copy-start.3
  234.0 2.2 copy-start.9
  236.2 1.7 copy-start.4
  249.8 4.6 %copy-start.2 = (f32[512,3072]{1,0:T(8,128)S(1)}, f32[512,3072]{1,0:T(8,128)}, u32[]{:S(2)}) copy-start(f32[512,3072]{1,0:T(8,128)} %fusion.114) | copy-start | bytes 18874372 | tf_op jit(solution)/shard_map/while
  254.4 1.9 copy-start.3
  256.3 2.2 copy-start.9
  258.5 1.7 copy-start.4
  272.2 4.6 %copy-start.2 = (f32[512,3072]{1,0:T(8,128)S(1)}, f32[512,3072]{1,0:T(8,128)}, u32[]{:S(2)}) copy-start(f32[512,3072]{1,0:T(8,128)} %fusion.114) | copy-start | bytes 18874372 | tf_op jit(solution)/shard_map/while
  276.8 1.9 copy-start.3
  278.7 2.2 copy-start.9
  280.8 1.7 copy-start.4
  286.2 2.4 copy-start.11
  288.6 1.2 copy-start.7
  291.5 31.0 %all-to-all-start.3 = ((bf16[8,512,256]{2,1,0:T(8,128)(2,1)}), bf16[8,512,256]{2,1,0:T(8,128)(2,1)}, u32[]{:S(2)}, u32[]{:S(2)}) async-start(bf16[8,512,256]{2,1,0:T(8,128)(2,1)} %copy.24), calls=%async_computation.3 | async-start | bytes 4194304 | tf_op jit(solution)/shard_map/all_to_all | solution.py:127
  297.9 1.2 copy-start.5
  322.5 31.0 %all-to-all-start.2 = ((bf16[8,512,256]{2,1,0:T(8,128)(2,1)}), bf16[8,512,256]{2,1,0:T(8,128)(2,1)}, u32[]{:S(2)}, u32[]{:S(2)}) async-start(bf16[8,512,256]{2,1,0:T(8,128)(2,1)} %copy.19), calls=%async_computation.2 | async-start | bytes 4194304 | tf_op jit(solution)/shard_map/all_to_all | solution.py:126
  327.1 3.0 copy-start.8
  353.5 3.0 copy-start.6
  356.5 2.9 copy-start.1
Sparse Core Ops, SparseCore 0:
  9.6 83.4 all-gather.1
where the time goes:
time: 368 us; the launch traced here: 366 us
  matrix products  135 us (37%)
  waiting for transfers between devices  64.6 us (18%)
  other arithmetic  54.8 us (15%)
  local copies, waits for them, and re-layouts  51.8 us (14%)
  blocking collectives  31.7 us (9%)
  between operations  14.2 us (4%)
  starting transfers between devices  13.3 us (4%)
    dot_general x8, matrix products, one_head(): jnp.dot(weights_low, value_head, preferred_element_type=jnp.float32)  33 us
    all_to_all x1, blocking collectives, shards(): lax.all_to_all(send_values, 'seq', split_axis=0, concat_axis=0, tiled=True)  31.7 us
    div x8, other arithmetic, one_head(): weights = shifted / jnp.sum(shifted, axis=1, keepdims=True)  31.4 us
    dot_general x8, matrix products, one_head(): lax.dot_general(weights_low, grad_head, (((0,), (0,)), ((), ())), preferr...  29.1 us
    all_to_all x1, waiting for transfers between devices, shards(): lax.all_to_all(back_values, 'seq', split_axis=0, concat_axis=0, tiled=True)  21.7 us
    all_to_all x1, waiting for transfers between devices, shards(): lax.all_to_all(back_keys, 'seq', split_axis=0, concat_axis=0, tiled=True)  20.5 us
    dot_general x8, matrix products, score_tile(): lax.dot_general(query_head, key_head, (((1,), (1,)), ((), ())), preferred...  18.8 us
    all_to_all x1, waiting for transfers between devices, shards(): lax.all_to_all(send_keys, 'seq', split_axis=0, concat_axis=0, tiled=True)  18.5 us
  transfers between devices with their start and end apart: 4, of which 4 were waited for; matrix products, arithmetic and copies ran while one was open for 10% of the time, Pallas kernels for 0%

commit v1 on v0

v1 whole, which is shorter than its diff:
```python
import functools
import math

import jax
import jax.numpy as jnp
from jax import lax
from jax.experimental import pallas as pl
from jax.experimental.pallas import tpu as pltpu
from jax.sharding import PartitionSpec as P


HEAD_DIM = 128
BLOCK = 512
TOPK = 6
CHUNKS = 2
HIDDEN = -1e30


HBM = pl.BlockSpec(memory_space=pltpu.HBM)
ANY = pl.BlockSpec(memory_space=pltpu.HBM)
SMEM = pl.BlockSpec(memory_space=pltpu.SMEM)
VMEM_LIMIT = 60 * 1024 * 1024
PARTS = 2
SPAN = 3
NT = (((1,), (1,)), ((), ()))


def pick_of(sel_ref, row, owner, blocks_here):
    found = jnp.int32(-1)
    for slot in range(TOPK):
        block = sel_ref[row, slot]
        found = jnp.where(block // blocks_here == owner, block % blocks_here, found)
    return found


def pack_kernel(head, devices, blocks_here, sel_ref, pos_ref, keys_ref, values_ref, out_ref, buf, in_sem, out_sem):
    here = pos_ref[0]
    cols = pl.ds(head * HEAD_DIM, HEAD_DIM)

    def loads(shift, inner):
        rows = pl.ds(pl.multiple_of(inner * BLOCK, BLOCK), BLOCK)
        slot = buf.at[shift]
        return (
            pltpu.make_async_copy(keys_ref.at[rows, cols], slot.at[pl.ds(0, BLOCK)], in_sem.at[shift, 0]),
            pltpu.make_async_copy(values_ref.at[rows, cols], slot.at[pl.ds(BLOCK, BLOCK)], in_sem.at[shift, 1]),
        )

    def store(shift):
        return pltpu.make_async_copy(buf.at[shift], out_ref.at[here + shift], out_sem.at[shift])

    for shift in range(1, devices):
        @pl.when(here + shift < devices)
        def _():
            inner = jnp.maximum(pick_of(sel_ref, here + shift, here, blocks_here), 0)
            for copy in loads(shift, inner):
                copy.start()

    for shift in range(1, devices):
        @pl.when(here + shift < devices)
        def _():
            for copy in loads(shift, 0):
                copy.wait()
            store(shift).start()

    for shift in range(1, devices):
        @pl.when(here + shift < devices)
        def _():
            store(shift).wait()


def pack(head, devices, blocks_here, selected, position, keys, values):
    shape = (devices, 2 * BLOCK, HEAD_DIM)
    return pl.pallas_call(
        functools.partial(pack_kernel, head, devices, blocks_here),
        out_shape=jax.ShapeDtypeStruct(shape, jnp.bfloat16),
        in_specs=[SMEM, SMEM, HBM, HBM],
        out_specs=HBM,
        scratch_shapes=[
            pltpu.VMEM(shape, jnp.bfloat16),
            pltpu.SemaphoreType.DMA((devices, 2)),
            pltpu.SemaphoreType.DMA((devices,)),
        ],
        compiler_params=pltpu.CompilerParams(vmem_limit_bytes=VMEM_LIMIT),
    )(selected, position, keys, values)


def project_kernel(terms, chunks, place_ref, *refs):
    count = len(terms)
    og_refs, weight_ref, acc, og_buf, w_buf, sem = refs[: count * chunks], *refs[count * chunks :]
    here, groups = place_ref[0], place_ref[1]
    rows, depth = og_buf.shape[1] // chunks, og_buf.shape[2]

    def present(term):
        source = here + terms[term]
        return source, (source >= 0) & (source < groups)

    def copies(term, source):
        cols = pl.ds(pl.multiple_of(source * depth, depth), depth)
        made = [pltpu.make_async_copy(weight_ref.at[:, cols], w_buf.at[term], sem.at[term, 0])]
        for chunk in range(chunks):
            made.append(
                pltpu.make_async_copy(
                    og_refs[term * chunks + chunk],
                    og_buf.at[term, pl.ds(chunk * rows, rows)],
                    sem.at[term, 1 + chunk],
                )
            )
        return made

    for term in range(count):
        source, there = present(term)

        @pl.when(there)
        def _():
            for copy in copies(term, source):
                copy.start()

    for term in range(count):
        source, there = present(term)

        @pl.when(there)
        def _():
            for copy in copies(term, 0):
                copy.wait()
            product = lax.dot_general(
                og_buf[term], w_buf[term], NT, preferred_element_type=jnp.float32
            )
            acc[...] = product if terms[term] == 0 else acc[...] + product


def project(terms, arrays, weight, place):
    chunks = len(arrays[0])
    rows, depth = arrays[0][0].shape
    out_cols = weight.shape[0]
    flat = [part for term in arrays for part in term]
    return pl.pallas_call(
        functools.partial(project_kernel, terms, chunks),
        out_shape=jax.ShapeDtypeStruct((rows * chunks, out_cols), jnp.float32),
        in_specs=[SMEM] + [ANY] * len(flat) + [HBM],
        out_specs=pl.BlockSpec(memory_space=pltpu.VMEM),
        scratch_shapes=[
            pltpu.VMEM((len(terms), rows * chunks, depth), jnp.bfloat16),
            pltpu.VMEM((len(terms), out_cols, depth), jnp.bfloat16),
            pltpu.SemaphoreType.DMA((len(terms), 1 + chunks)),
        ],
        compiler_params=pltpu.CompilerParams(vmem_limit_bytes=VMEM_LIMIT),
        name="project",
    )(place, *flat, weight)


def weigh_kernel(head, blocks_here, has_old, *refs):
    sel_ref, pos_ref, q_ref, keys_ref, values_ref, recv_ref = refs[:6]
    refs = refs[11:] if has_old else refs[6:]
    p_ref, o_ref, i_ref, k_out, v_out, k_buf, v_buf, in_sem, out_sem = refs
    here = pos_ref[0]
    step = pl.program_id(0)
    rows = q_ref.shape[0]
    to_log2 = HEAD_DIM ** (-0.5) * math.log2(math.e)
    cols = pl.ds(head * HEAD_DIM, HEAD_DIM)

    def fetch(slot, key_src, value_src):
        where = pl.ds(slot * BLOCK, BLOCK)
        return (
            pltpu.make_async_copy(key_src, k_buf.at[where], in_sem.at[slot, 0]),
            pltpu.make_async_copy(value_src, v_buf.at[where], in_sem.at[slot, 1]),
        )

    def keep():
        return (
            pltpu.make_async_copy(k_buf, k_out.at[head], out_sem.at[0]),
            pltpu.make_async_copy(v_buf, v_out.at[head], out_sem.at[1]),
        )

    @pl.when(step == 0)
    def _():
        for slot in range(TOPK):
            block = sel_ref[here, slot]
            dist = here - block // blocks_here

            @pl.when(dist == 0)
            def _():
                src = pl.ds(pl.multiple_of(block % blocks_here * BLOCK, BLOCK), BLOCK)
                for copy in fetch(slot, keys_ref.at[src, cols], values_ref.at[src, cols]):
                    copy.start()

            if slot > 0:
                @pl.when(dist != 0)
                def _():
                    arrived = recv_ref.at[here - dist]
                    for copy in fetch(slot, arrived.at[pl.ds(0, BLOCK)], arrived.at[pl.ds(BLOCK, BLOCK)]):
                        copy.start()

        for slot in range(TOPK):
            first = pl.ds(0, BLOCK)
            for copy in fetch(slot, keys_ref.at[first, cols], values_ref.at[first, cols]):
                copy.wait()
        for copy in keep():
            copy.start()

    tile = rows // PARTS
    for part in range(PARTS):
        at = pl.ds(part * tile, tile)
        row = lax.broadcasted_iota(jnp.int32, (tile, BLOCK), 0) + part * tile
        visible = lax.broadcasted_iota(jnp.int32, (tile, BLOCK), 1) <= row
        scores = lax.dot_general(q_ref[at, :], k_buf[...], NT, preferred_element_type=jnp.float32)
        first = jnp.where(visible, scores[:, :BLOCK], HIDDEN)
        top = jnp.maximum(
            jnp.max(first, axis=1, keepdims=True), jnp.max(scores[:, BLOCK:], axis=1, keepdims=True)
        )
        total = jnp.zeros((tile, HEAD_DIM), jnp.float32)
        for slot in range(TOPK):
            piece = first if slot == 0 else scores[:, slot * BLOCK : (slot + 1) * BLOCK]
            raised = jnp.exp2((piece - top) * to_log2)
            for lane in range(BLOCK // HEAD_DIM):
                total = total + raised[:, lane * HEAD_DIM : (lane + 1) * HEAD_DIM]
            p_ref[0, slot, 0, at, :] = raised.astype(jnp.bfloat16)
        inverse = 1.0 / jnp.sum(total, axis=1, keepdims=True)
        attended = jnp.zeros((tile, HEAD_DIM), jnp.float32)
        for slot in range(TOPK):
            attended = attended + jnp.dot(
                p_ref[0, slot, 0, at, :], v_buf[pl.ds(slot * BLOCK, BLOCK), :], preferred_element_type=jnp.float32
            )
        o_ref[at, :] = attended * inverse
        i_ref[at, :] = jnp.broadcast_to(inverse, (tile, HEAD_DIM))

    @pl.when(step == pl.num_programs(0) - 1)
    def _():
        for copy in keep():
            copy.wait()


def weigh(head, kv_local, blocks_here, selected, position, queries, keys, values, recv, old):
    rows, q_cols = queries.shape
    group = q_cols // kv_local // HEAD_DIM
    length = TOPK * BLOCK
    slots = jax.ShapeDtypeStruct((kv_local, length, HEAD_DIM), jnp.bfloat16)
    wide = jax.ShapeDtypeStruct((rows, q_cols), jnp.float32)
    head_block = pl.BlockSpec((rows, HEAD_DIM), lambda g: (0, head * group + g))
    operands = [selected, position, queries, keys, values, recv]
    in_specs = [SMEM, SMEM, head_block, HBM, HBM, ANY]
    aliases = {}
    if old is not None:
        aliases = {len(operands) + n: n for n in range(5)}
        operands += list(old)
        in_specs += [HBM] * 5
    return pl.pallas_call(
        functools.partial(weigh_kernel, head, blocks_here, old is not None),
        grid=(group,),
        out_shape=[
            jax.ShapeDtypeStruct((kv_local, TOPK, group, rows, BLOCK), jnp.bfloat16), wide, wide, slots, slots,
        ],
        in_specs=in_specs,
        out_specs=[
            pl.BlockSpec((1, TOPK, 1, rows, BLOCK), lambda g: (head, 0, g, 0, 0)),
            head_block, head_block, HBM, HBM,
        ],
        scratch_shapes=[
            pltpu.VMEM((length, HEAD_DIM), jnp.bfloat16),
            pltpu.VMEM((length, HEAD_DIM), jnp.bfloat16),
            pltpu.SemaphoreType.DMA((TOPK, 2)),
            pltpu.SemaphoreType.DMA((2,)),
        ],
        input_output_aliases=aliases,
        compiler_params=pltpu.CompilerParams(vmem_limit_bytes=VMEM_LIMIT),
    )(*operands)


def send_piece(step, here, sel_ref, blocks_here, piece, back_ref, local_ref, sem):
    head, slot = step // TOPK, step % TOPK
    rows = pl.ds(pl.multiple_of(head * BLOCK, BLOCK), BLOCK)
    dist = here - sel_ref[here, slot] // blocks_here

    @pl.when(dist == 0)
    def _():
        pltpu.make_async_copy(piece.at[step], local_ref.at[slot, rows], sem.at[step]).start()

    @pl.when(dist != 0)
    def _():
        pltpu.make_async_copy(piece.at[step], back_ref.at[here - dist, rows], sem.at[step]).start()

    @pl.when(step == piece.shape[0] - 1)
    def _():
        for index in range(piece.shape[0]):
            pltpu.make_async_copy(piece.at[index], local_ref.at[0, pl.ds(0, BLOCK)], sem.at[index]).wait()


def values_kernel(blocks_here, group, chunks, late, *refs):
    sel_ref, pos_ref, place_ref, total_ref, i_ref = refs[:5]
    p_refs, refs = refs[5 : 5 + group], refs[5 + group :]
    if late:
        og_above, og_below, weight_ref = refs[:chunks], refs[chunks : 2 * chunks], refs[2 * chunks]
        refs = refs[2 * chunks + 1 :]
    go_ref, back_ref, local_ref, go_t, piece, og_buf, w_buf, late_sem, out_sem = refs
    here = pos_ref[0]
    step = pl.program_id(0)
    rows, width = total_ref.shape

    if late:
        z, groups = place_ref[0], place_ref[1]
        depth = og_buf.shape[1]
        size = rows // chunks

        def copies(arrays, source):
            cols = pl.ds(pl.multiple_of(source * depth, depth), depth)
            made = [pltpu.make_async_copy(weight_ref.at[:, cols], w_buf, late_sem.at[chunks])]
            for c in range(chunks):
                made.append(pltpu.make_async_copy(arrays[c], og_buf.at[pl.ds(c * size, size)], late_sem.at[c]))
            return made

        ends = (z == 0) | (z == groups - 1)

        @pl.when((step == 0) & (z == 0))
        def _():
            for copy in copies(og_above, groups - 1):
                copy.start()

        @pl.when((step == 0) & (z == groups - 1))
        def _():
            for copy in copies(og_below, 0):
                copy.start()

        @pl.when((step == 0) & ends)
        def _():
            for copy in copies(og_above, 0):
                copy.wait()

    def store(grad):
        low = (grad * i_ref[...]).astype(jnp.bfloat16)
        go_ref[...] = low
        for g in range(group):
            go_t[:, pl.ds(g * rows, rows)] = low[:, g * HEAD_DIM : (g + 1) * HEAD_DIM].T

    @pl.when(step * SPAN % TOPK == 0)
    def _():
        if late:
            @pl.when(ends)
            def _():
                mine = pl.ds(pl.multiple_of(step * SPAN // TOPK * width, width), width)
                store(
                    total_ref[...]
                    + lax.dot_general(og_buf[...], w_buf[mine, :], NT, preferred_element_type=jnp.float32)
                )

            @pl.when(jnp.logical_not(ends))
            def _():
                store(total_ref[...])
        else:
            store(total_ref[...])

    for part in range(SPAN):
        value_part = jnp.zeros((HEAD_DIM, BLOCK), jnp.float32)
        for g in range(group):
            value_part = value_part + jnp.dot(
                go_t[:, g * rows : (g + 1) * rows], p_refs[g][0, part, 0], preferred_element_type=jnp.float32
            )
        piece[step * SPAN + part] = value_part.T.astype(jnp.bfloat16)
    for part in range(SPAN):
        send_piece(step * SPAN + part, here, sel_ref, blocks_here, piece, back_ref, local_ref, out_sem)


def shapes_back(devices, kv_local):
    tall = kv_local * BLOCK
    return [
        jax.ShapeDtypeStruct((devices, tall, HEAD_DIM), jnp.bfloat16),
        jax.ShapeDtypeStruct((TOPK, tall, HEAD_DIM), jnp.bfloat16),
    ]


def weight_blocks(group, rows, span):
    return [
        pl.BlockSpec(
            (1, span, 1, rows, BLOCK),
            functools.partial(lambda g, s: (s * span // TOPK, s % (TOPK // span), g, 0, 0), g),
        )
        for g in range(group)
    ]


def value_grads(kv_local, devices, blocks_here, selected, position, place, total, weighed, late, weight):
    rows, q_cols = total.shape
    width = q_cols // kv_local
    group = width // HEAD_DIM
    weights, _, inverse, _, _ = weighed
    column_block = pl.BlockSpec((rows, width), lambda s: (0, s * SPAN // TOPK))
    operands = [selected, position, place, total, inverse] + [weights] * group
    in_specs = [
        SMEM, SMEM, SMEM, column_block, column_block, *weight_blocks(group, rows, SPAN),
    ]
    chunks, depth = 1, HEAD_DIM
    if late is not None:
        chunks, depth = len(late[0]), late[0][0].shape[1]
        extra = [*late[0], *late[1], weight]
        operands += extra
        in_specs += [ANY] * (len(extra) - 1) + [HBM]
    steps = kv_local * TOPK
    return pl.pallas_call(
        functools.partial(values_kernel, blocks_here, group, chunks, late is not None),
        grid=(steps // SPAN,),
        out_shape=[jax.ShapeDtypeStruct((rows, q_cols), jnp.bfloat16)] + shapes_back(devices, kv_local),
        in_specs=in_specs,
        out_specs=[column_block, HBM, HBM],
        scratch_shapes=[
            pltpu.VMEM((HEAD_DIM, group * rows), jnp.bfloat16),
            pltpu.VMEM((steps, BLOCK, HEAD_DIM), jnp.bfloat16),
            pltpu.VMEM((rows, depth), jnp.bfloat16),
            pltpu.VMEM((q_cols, depth), jnp.bfloat16),
            pltpu.SemaphoreType.DMA((chunks + 1,)),
            pltpu.SemaphoreType.DMA((steps,)),
        ],
        compiler_params=pltpu.CompilerParams(vmem_limit_bytes=VMEM_LIMIT),
        name="values",
    )(*operands)


def keys_kernel(blocks_here, group, *refs):
    sel_ref, pos_ref, q_ref, go_ref, o_ref, k_ref, v_ref = refs[:7]
    p_refs, refs = refs[7 : 7 + group], refs[7 + group :]
    dq_ref, back_ref, local_ref, q_t, dot_buf, ds_buf, dq_acc, piece, out_sem = refs
    here = pos_ref[0]
    step = pl.program_id(0)
    rows, _ = q_ref.shape
    factor = HEAD_DIM ** (-0.5)

    @pl.when(step % TOPK == 0)
    def _():
        for g in range(group):
            at = slice(g * HEAD_DIM, (g + 1) * HEAD_DIM)
            q_t[:, pl.ds(g * rows, rows)] = q_ref[:, at].T
            row_dot = jnp.sum(go_ref[:, at].astype(jnp.float32) * o_ref[:, at], axis=1, keepdims=True)
            dot_buf[g] = jnp.broadcast_to(row_dot, (rows, HEAD_DIM))
        dq_acc[...] = jnp.zeros_like(dq_acc)

    keys_here = k_ref[0]
    values_here = v_ref[0]

    def grad_weights(g):
        return lax.dot_general(
            go_ref[:, g * HEAD_DIM : (g + 1) * HEAD_DIM], values_here, NT, preferred_element_type=jnp.float32
        )

    later = grad_weights(0)
    for g in range(group):
        at = slice(g * HEAD_DIM, (g + 1) * HEAD_DIM)
        now = later
        if g + 1 < group:
            later = grad_weights(g + 1)
        row_dot = jnp.concatenate([dot_buf[g]] * (BLOCK // HEAD_DIM), axis=1)
        grad_low = (p_refs[g][0, 0, 0].astype(jnp.float32) * (now - row_dot)).astype(jnp.bfloat16)
        ds_buf[pl.ds(g * rows, rows)] = grad_low
        dq_acc[:, at] += jnp.dot(grad_low, keys_here, preferred_element_type=jnp.float32)
    key_part = jnp.dot(q_t[...], ds_buf[...], preferred_element_type=jnp.float32)
    piece[step] = (key_part.T * factor).astype(jnp.bfloat16)

    @pl.when(step % TOPK == TOPK - 1)
    def _():
        dq_ref[...] = (dq_acc[...] * factor).astype(jnp.bfloat16)

    send_piece(step, here, sel_ref, blocks_here, piece, back_ref, local_ref, out_sem)


def key_grads(kv_local, devices, blocks_here, selected, position, queries, grad_output, weighed):
    rows, q_cols = queries.shape
    width = q_cols // kv_local
    group = width // HEAD_DIM
    weights, attended, _, key_slots, value_slots = weighed
    column_block = pl.BlockSpec((rows, width), lambda s: (0, s // TOPK))
    slot_block = pl.BlockSpec((1, BLOCK, HEAD_DIM), lambda s: (s // TOPK, s % TOPK, 0))
    steps = kv_local * TOPK
    return pl.pallas_call(
        functools.partial(keys_kernel, blocks_here, group),
        grid=(steps,),
        out_shape=[jax.ShapeDtypeStruct((rows, q_cols), jnp.bfloat16)] + shapes_back(devices, kv_local),
        in_specs=[
            SMEM, SMEM, column_block, column_block, column_block, slot_block, slot_block,
            *weight_blocks(group, rows, 1),
        ],
        out_specs=[column_block, HBM, HBM],
        scratch_shapes=[
            pltpu.VMEM((HEAD_DIM, group * rows), jnp.bfloat16),
            pltpu.VMEM((group, rows, HEAD_DIM), jnp.float32),
            pltpu.VMEM((group * rows, BLOCK), jnp.bfloat16),
            pltpu.VMEM((rows, width), jnp.float32),
            pltpu.VMEM((steps, BLOCK, HEAD_DIM), jnp.bfloat16),
            pltpu.SemaphoreType.DMA((steps,)),
        ],
        compiler_params=pltpu.CompilerParams(vmem_limit_bytes=VMEM_LIMIT),
        name="keys",
    )(selected, position, queries, grad_output, attended, key_slots, value_slots, *[weights] * group)


def collect_kernel(kv_local, devices, blocks_here, sel_ref, pos_ref, local_ref, recv_ref, out_ref, pieces, acc, low, in_sem, out_sem):
    here = pos_ref[0]
    total = TOPK + devices - 1

    def source(index):
        if index < TOPK:
            block = sel_ref[here, index]
            return block % blocks_here, block // blocks_here == here
        row = here + (index - TOPK + 1)
        inner = pick_of(sel_ref, jnp.minimum(row, devices - 1), here, blocks_here)
        return inner, (row < devices) & (inner >= 0)

    def fetch(index):
        src = local_ref.at[index] if index < TOPK else recv_ref.at[here + (index - TOPK + 1)]
        return pltpu.make_async_copy(src, pieces.at[index], in_sem.at[index])

    for index in range(total):
        @pl.when(source(index)[1])
        def _():
            fetch(index).start()

    acc[...] = jnp.zeros_like(acc)
    for index in range(total):
        inner, there = source(index)

        @pl.when(there)
        def _():
            fetch(index).wait()
            acc[inner] += pieces[index].astype(jnp.float32)

    def store(block):
        rows = pl.ds(block * BLOCK, BLOCK)
        return [
            pltpu.make_async_copy(
                low.at[block, pl.ds(head * BLOCK, BLOCK)],
                out_ref.at[rows, pl.ds(head * HEAD_DIM, HEAD_DIM)],
                out_sem.at[block, head],
            )
            for head in range(kv_local)
        ]

    for block in range(blocks_here):
        low[block] = acc[block].astype(jnp.bfloat16)
        for copy in store(block):
            copy.start()
    for block in range(blocks_here):
        for copy in store(block):
            copy.wait()


def collect(kv_local, devices, blocks_here, selected, position, local, recv):
    tall = kv_local * BLOCK
    return pl.pallas_call(
        functools.partial(collect_kernel, kv_local, devices, blocks_here),
        out_shape=jax.ShapeDtypeStruct((blocks_here * BLOCK, kv_local * HEAD_DIM), jnp.bfloat16),
        in_specs=[SMEM, SMEM, HBM, ANY],
        out_specs=HBM,
        scratch_shapes=[
            pltpu.VMEM((TOPK + devices - 1, tall, HEAD_DIM), jnp.bfloat16),
            pltpu.VMEM((blocks_here, tall, HEAD_DIM), jnp.float32),
            pltpu.VMEM((blocks_here, tall, HEAD_DIM), jnp.bfloat16),
            pltpu.SemaphoreType.DMA((TOPK + devices - 1,)),
            pltpu.SemaphoreType.DMA((blocks_here, kv_local)),
        ],
        compiler_params=pltpu.CompilerParams(vmem_limit_bytes=VMEM_LIMIT),
    )(selected, position, local, recv)


def body(queries, keys, values, out_grad, out_weight, selected):
    kv_cols = keys.shape[1]
    kv_local = kv_cols // HEAD_DIM
    blocks_here = keys.shape[0] // BLOCK
    devices = lax.axis_size("seq")
    groups = lax.axis_size("head")
    position = lax.axis_index("seq").astype(jnp.int32).reshape(1)
    place = jnp.stack([lax.axis_index("head"), jnp.int32(groups)]).astype(jnp.int32)

    rows = out_grad.shape[0] // CHUNKS
    own = [out_grad[c * rows : (c + 1) * rows] for c in range(CHUNKS)]
    above, below = {0: own}, {0: own}
    for step in range(1, groups):
        up = [(z, z + 1) for z in range(step - 1, groups - 1)]
        down = [(z, z - 1) for z in range(1, groups - step + 1)]
        below[step], above[step] = [], []
        for c in range(CHUNKS):
            below[step].append(lax.ppermute(below[step - 1][c], "head", up))
            above[step].append(lax.ppermute(above[step - 1][c], "head", down))

    def trade(array):
        return lax.all_to_all(array, "seq", split_axis=0, concat_axis=0, tiled=True)

    recv = [trade(pack(head, devices, blocks_here, selected, position, keys, values)) for head in range(kv_local)]

    early = [0] + [t for s in range(1, groups - 1) for t in (-s, s)]
    arrays = [below[-t] if t < 0 else above[t] for t in early]
    total = project(tuple(early), arrays, out_weight, place)
    late = (above[groups - 1], below[groups - 1]) if groups > 1 else None
    weighed = None
    for head in range(kv_local):
        weighed = weigh(head, kv_local, blocks_here, selected, position, queries, keys, values, recv[head], weighed)

    grad_output, back_values, local_values = value_grads(
        kv_local, devices, blocks_here, selected, position, place, total, weighed, late, out_weight
    )
    arrived_values = trade(back_values)
    query_grad, back_keys, local_keys = key_grads(
        kv_local, devices, blocks_here, selected, position, queries, grad_output, weighed
    )
    arrived_keys = trade(back_keys)
    value_grad = collect(kv_local, devices, blocks_here, selected, position, local_values, arrived_values)
    key_grad = collect(kv_local, devices, blocks_here, selected, position, local_keys, arrived_keys)
    return (query_grad, key_grad, value_grad)


def solution(mesh):
    in_specs = (
        P("seq", "head"),
        P("seq", "head"),
        P("seq", "head"),
        P("seq", "head"),
        P("head", None),
        P(),
    )
    out_specs = (P("seq", "head"), P("seq", "head"), P("seq", "head"))
    return jax.shard_map(body, mesh=mesh, in_specs=in_specs, out_specs=out_specs, check_vma=False)
```

time: 368 us -> 228 us (0.62)
  matrix products: 135 us -> 0 us
  Pallas kernels: 0 us -> 96.4 us
  other arithmetic: 54.8 us -> 0.59 us
  local copies, waits for them, and re-layouts: 51.8 us -> 5.23 us
  blocking collectives: 31.7 us -> 0 us
  starting transfers between devices: 13.3 us -> 37.6 us
  waiting for transfers between devices: 64.6 us -> 86.5 us
  between operations: 14.2 us -> 1.04 us
    dot_general x55 -> x0, matrix products: 135 us -> none  [the longest x8 33 us: one_head(): jnp.dot(weights_low, value_head, preferred_element_type=jnp.float32)]
    pallas_call x0 -> x9, Pallas kernels: none -> 96.4 us  [the longest x2 29.9 us: weigh(): pl.pallas_call(functools.partial(weigh_kernel, head, blocks_here, old is...]
    ppermute x0 -> x12, waiting for transfers between devices: none -> 40.4 us  [the longest x6 25.1 us: body(): above[step].append(lax.ppermute(above[step - 1][c], 'head', down))]
    all_to_all x1 -> x0, blocking collectives: 31.7 us -> none  [shards(): lax.all_to_all(send_values, 'seq', split_axis=0, concat_axis=0, tiled=True)]
    div x8 -> x0, other arithmetic: 31.4 us -> none  [one_head(): weights = shifted / jnp.sum(shifted, axis=1, keepdims=True)]
    ppermute x0 -> x12, starting transfers between devices: none -> 21 us  [the longest x6 13.3 us: body(): below[step].append(lax.ppermute(below[step - 1][c], 'head', up))]
    gather x6 -> x0, local copies, waits for them, and re-layouts: 16.3 us -> none  [the longest x2 5.48 us: assemble(): local_rows = jnp.take(local_tiles, my_inner, axis=0)]
    while x64 -> x0, local copies, waits for them, and re-layouts: 16.1 us -> none
  transfers between devices with their start and end apart: 4 -> 16, of which waited for: 4 -> 8; matrix products, arithmetic and copies ran while one was open for 10% -> 1% of each run, Pallas kernels for 0% -> 32%
where the time goes in v1:
time: 228 us; the launch traced here: 227 us
  Pallas kernels  96.4 us (42%)
  waiting for transfers between devices  86.5 us (38%)
  starting transfers between devices  37.6 us (16%)
  local copies, waits for them, and re-layouts  5.23 us (2%)
    all_to_all x4, waiting for transfers between devices, trade(): return lax.all_to_all(array, 'seq', split_axis=0, concat_axis=0, tiled=True)  46 us
    pallas_call x2, Pallas kernels, weigh(): pl.pallas_call(functools.partial(weigh_kernel, head, blocks_here, old is...  29.9 us
    pallas_call x1, Pallas kernels, key_grads(): pl.pallas_call(functools.partial(keys_kernel, blocks_here, group), grid=(...  26.2 us
    ppermute x6, waiting for transfers between devices, body(): above[step].append(lax.ppermute(above[step - 1][c], 'head', down))  25.1 us
    pallas_call x1, Pallas kernels, value_grads(): pl.pallas_call(functools.partial(values_kernel, blocks_here, group, chunk...  17.1 us
    all_to_all x4, starting transfers between devices, trade(): return lax.all_to_all(array, 'seq', split_axis=0, concat_axis=0, tiled=True)  16.7 us
    ppermute x6, waiting for transfers between devices, body(): below[step].append(lax.ppermute(below[step - 1][c], 'head', up))  15.4 us
    ppermute x6, starting transfers between devices, body(): below[step].append(lax.ppermute(below[step - 1][c], 'head', up))  13.3 us
  transfers between devices with their start and end apart: 16, of which 8 were waited for; matrix products, arithmetic and copies ran while one was open for 1% of the time, Pallas kernels for 32%

profile of v1, /device:TPU:0, one launch (start us, length us, event | category | flops | bytes accessed | tf_op | source)
XLA Modules:
  0.0 227.4 jit_solution(15707550898108956212)
XLA Ops:
  0.6 3.3 %shard_map.86 = bf16[8,1024,128]{2,1,0:T(8,128)(2,1)} custom-call(s32[8,6]{1,0:T(8,128)} %sel_ref.7, s32[1]{0:T(128)} %bitcast.pos_ref.refs_1_, bf16[4096,256]{1,0:T(8,128)(2,1)} %refs_3_.3, bf16[4096,256]{1,0:T(8,128)(2,1)} %refs_4_.3), custom_call_target="tpu_custom_call" | custom-call | tf_op jit(solution)/shard_map/pallas_call | solution.py:73
  3.9 4.6 %all-to-all-start.1 = ((bf16[8,1024,128]{2,1,0:T(8,128)(2,1)}), bf16[8,1024,128]{2,1,0:T(8,128)(2,1)S(1)}, u32[]{:S(2)}, u32[]{:S(2)}) async-start(bf16[8,1024,128]{2,1,0:T(8,128)(2,1)} %shard_map.86), calls=%async_computation.1 | async-start | bytes 4194304 | tf_op jit(solution)/shard_map/all_to_all | solution.py:580
  8.5 3.3 %shard_map.85 = bf16[8,1024,128]{2,1,0:T(8,128)(2,1)} custom-call(s32[8,6]{1,0:T(8,128)} %sel_ref.7, s32[1]{0:T(128)} %bitcast.pos_ref.refs_1_, bf16[4096,256]{1,0:T(8,128)(2,1)} %refs_3_.3, bf16[4096,256]{1,0:T(8,128)(2,1)} %refs_4_.3), custom_call_target="tpu_custom_call" | custom-call | tf_op jit(solution)/shard_map/pallas_call | solution.py:73
  11.8 23.4 %all-to-all-done.1.refs_5_ = bf16[8,1024,128]{2,1,0:T(8,128)(2,1)S(1)} async-done(((bf16[8,1024,128]{2,1,0:T(8,128)(2,1)}), bf16[8,1024,128]{2,1,0:T(8,128)(2,1)S(1)}, u32[]{:S(2)}, u32[]{:S(2)}) %all-to-all-start.1) | async-done | bytes 2097184 | tf_op jit(solution)/shard_map/all_to_all | solution.py:580
  35.1 0.0 copy-start.1
  35.1 1.3 copy-done.1
  36.4 3.6 %all-to-all-start = ((bf16[8,1024,128]{2,1,0:T(8,128)(2,1)}), bf16[8,1024,128]{2,1,0:T(8,128)(2,1)S(1)}, u32[]{:S(2)}, u32[]{:S(2)}) async-start(bf16[8,1024,128]{2,1,0:T(8,128)(2,1)} %shard_map.85), calls=%async_computation | async-start | bytes 4194304 | tf_op jit(solution)/shard_map/all_to_all | solution.py:580
  40.0 1.3 fusion
  41.3 0.0 copy-start.3
  41.3 0.0 copy-start.4
  41.3 3.9 %collective-permute-start = (bf16[256,1024]{1,0:T(8,128)(2,1)S(1)}, bf16[256,1024]{1,0:T(8,128)(2,1)S(1)}, u32[]{:S(2)}, u32[]{:S(2)}) collective-permute-start(bf16[256,1024]{1,0:T(8,128)(2,1)S(1)} %get-tuple-element.36.refs_0_), channel_id=1, source_target_pairs={{0,1},{1,2},{2,3},{4,5},{5,6},{6,7},{8,9},{9,10},{10,11},{12,13},{... | collective-permute-start | bytes 1572872 | tf_op jit(solution)/shard_map/ppermute | solution.py:576
  45.3 3.5 %collective-permute-start.1 = (bf16[256,1024]{1,0:T(8,128)(2,1)S(1)}, bf16[256,1024]{1,0:T(8,128)(2,1)S(1)}, u32[]{:S(2)}, u32[]{:S(2)}) collective-permute-start(bf16[256,1024]{1,0:T(8,128)(2,1)S(1)} %get-tuple-element.35.refs_1_), channel_id=1, source_target_pairs={{0,1},{1,2},{2,3},{4,5},{5,6},{6,7},{8,9},{9,10},{10,11},{12,13},{... | collective-permute-start | bytes 1572872 | tf_op jit(solution)/shard_map/ppermute | solution.py:576
  48.8 1.3 collective-permute-start.2
  50.1 1.3 collective-permute-start.3
  51.4 6.2 %collective-permute-done.refs_2_ = bf16[256,1024]{1,0:T(8,128)(2,1)S(1)} collective-permute-done((bf16[256,1024]{1,0:T(8,128)(2,1)S(1)}, bf16[256,1024]{1,0:T(8,128)(2,1)S(1)}, u32[]{:S(2)}, u32[]{:S(2)}) %collective-permute-start) | collective-permute-done | bytes 524320 | tf_op jit(solution)/shard_map/ppermute | solution.py:576
  57.5 0.0 copy-start.5
  57.5 1.5 collective-permute-start.4
  59.0 9.2 %collective-permute-done.1.refs_3_ = bf16[256,1024]{1,0:T(8,128)(2,1)S(1)} collective-permute-done((bf16[256,1024]{1,0:T(8,128)(2,1)S(1)}, bf16[256,1024]{1,0:T(8,128)(2,1)S(1)}, u32[]{:S(2)}, u32[]{:S(2)}) %collective-permute-start.1) | collective-permute-done | bytes 524320 | tf_op jit(solution)/shard_map/ppermute | solution.py:576
  68.2 0.0 copy-start.6
  68.2 1.5 collective-permute-start.5
  69.7 0.0 collective-permute-done.2.refs_4_
  69.7 0.0 copy-start.7
  69.7 1.3 collective-permute-start.6
  71.0 4.6 %collective-permute-done.3.refs_5_ = bf16[256,1024]{1,0:T(8,128)(2,1)S(1)} collective-permute-done((bf16[256,1024]{1,0:T(8,128)(2,1)S(1)}, bf16[256,1024]{1,0:T(8,128)(2,1)S(1)}, u32[]{:S(2)}, u32[]{:S(2)}) %collective-permute-start.3) | collective-permute-done | bytes 524320 | tf_op jit(solution)/shard_map/ppermute | solution.py:577
  75.6 0.0 copy-done.5
  75.6 0.0 copy-start.8
  75.6 1.3 collective-permute-start.7
  76.9 0.0 collective-permute-done.4.refs_6_
  76.9 0.0 copy-done.6
  76.9 1.5 collective-permute-start.10
  78.4 0.0 collective-permute-done.5.refs_7_
  78.4 0.0 copy-done.7
  78.4 1.5 collective-permute-start.11
  79.8 10.5 %collective-permute-done.6.refs_8_ = bf16[256,1024]{1,0:T(8,128)(2,1)} collective-permute-done((bf16[256,1024]{1,0:T(8,128)(2,1)S(1)}, bf16[256,1024]{1,0:T(8,128)(2,1)}, u32[]{:S(2)}, u32[]{:S(2)}) %collective-permute-start.6) | collective-permute-done | bytes 524320 | tf_op jit(solution)/shard_map/ppermute | solution.py:577
  90.3 0.0 copy-done.8
  90.3 1.3 collective-permute-start.8
  91.6 9.9 %collective-permute-done.7.refs_9_ = bf16[256,1024]{1,0:T(8,128)(2,1)} collective-permute-done((bf16[256,1024]{1,0:T(8,128)(2,1)S(1)}, bf16[256,1024]{1,0:T(8,128)(2,1)}, u32[]{:S(2)}, u32[]{:S(2)}) %collective-permute-start.7) | collective-permute-done | bytes 524320 | tf_op jit(solution)/shard_map/ppermute | solution.py:577
  101.5 1.3 collective-permute-start.9
  102.8 0.6 pad_add_fusion.place_ref.refs_2_
  103.4 0.0 copy-done.3
  103.4 0.0 copy-done.4
  103.4 8.0 %project.1.refs_3_ = f32[512,1024]{1,0:T(8,128)} custom-call(s32[2]{0:T(128)} %pad_add_fusion.place_ref.refs_2_, bf16[256,1024]{1,0:T(8,128)(2,1)} %copy-done.4, bf16[256,1024]{1,0:T(8,128)(2,1)} %copy-done.3, bf16[256,1024]{1,0:T(8,128)(2,1)} %copy-done.5, bf16[256,1024]{1,0:T(8,128)(2,1)} %copy-done.6, bf16[256,1024]{1,0:T(8,128)(2,1)} %copy-done.7, ...), custom_call_target="tpu_custom_call" | custom-call | tf_op jit(solution)/shard_map/project/pallas_call | solution.py:136
  111.5 14.9 %shard_map.87 = (bf16[2,6,4,512,512]{4,3,2,1,0:T(8,128)(2,1)}, f32[512,1024]{1,0:T(8,128)}, f32[512,1024]{1,0:T(8,128)}, bf16[2,3072,128]{2,1,0:T(8,128)(2,1)}, bf16[2,3072,128]{2,1,0:T(8,128)(2,1)}) custom-call(s32[8,6]{1,0:T(8,128)} %sel_ref.7, s32[1]{0:T(128)} %bitcast.pos_ref.refs_1_, bf16[512,1024]{1,0:T(8,128)(2,1)} %refs_2_.5, ...), custom_call_target="tpu_custom_call" | custom-call | tf_op jit(solution)/shard_map/pallas_call | solution.py:246
  126.4 0.0 all-to-all-done.refs_5_
  126.4 0.0 copy-start
  126.4 1.3 copy-done
  127.7 15.0 %shard_map.88 = (bf16[2,6,4,512,512]{4,3,2,1,0:T(8,128)(2,1)}, f32[512,1024]{1,0:T(8,128)}, f32[512,1024]{1,0:T(8,128)}, bf16[2,3072,128]{2,1,0:T(8,128)(2,1)}, bf16[2,3072,128]{2,1,0:T(8,128)(2,1)}) custom-call(s32[8,6]{1,0:T(8,128)} %sel_ref.7, ...), custom_call_target="tpu_custom_call", output_to_operand_aliasing={{0}: (6, {}), {1}: (7, {}), {2}: (8, {}), {3}: (9, {}), {4}... | custom-call | tf_op jit(solution)/shard_map/pallas_call | solution.py:246
  142.7 0.0 collective-permute-done.10.refs_11_
  142.7 0.0 collective-permute-done.11.refs_12_
  142.7 0.0 collective-permute-done.8.refs_9_
  142.8 0.0 collective-permute-done.9.refs_10_
  142.8 17.1 %values.1 = (bf16[512,1024]{1,0:T(8,128)(2,1)}, bf16[8,1024,128]{2,1,0:T(8,128)(2,1)}, bf16[6,1024,128]{2,1,0:T(8,128)(2,1)}) custom-call(s32[8,6]{1,0:T(8,128)} %sel_ref.7, s32[1]{0:T(128)} %bitcast.pos_ref.refs_1_, s32[2]{0:T(128)} %pad_add_fusion.place_ref.refs_2_, f32[512,1024]{1,0:T(8,128)} %project.1.refs_3_, f32[512,1024]{1,0:T(8,128)} %get-tuple-element.24.refs_4_, ...), custom_call_target="tpu_custom_call" | custom-call | tf_op jit(solution)/shard_map/values/pallas_call | solution.py:396
  159.9 4.1 %all-to-all-start.3 = ((bf16[8,1024,128]{2,1,0:T(8,128)(2,1)}), bf16[8,1024,128]{2,1,0:T(8,128)(2,1)S(1)}, u32[]{:S(2)}, u32[]{:S(2)}) async-start(bf16[8,1024,128]{2,1,0:T(8,128)(2,1)} %get-tuple-element.34), calls=%async_computation.3 | async-start | bytes 4194304 | tf_op jit(solution)/shard_map/all_to_all | solution.py:580
  164.0 26.2 %keys.1 = (bf16[512,1024]{1,0:T(8,128)(2,1)}, bf16[8,1024,128]{2,1,0:T(8,128)(2,1)}, bf16[6,1024,128]{2,1,0:T(8,128)(2,1)}) custom-call(s32[8,6]{1,0:T(8,128)} %sel_ref.7, s32[1]{0:T(128)} %bitcast.pos_ref.refs_1_, bf16[512,1024]{1,0:T(8,128)(2,1)} %refs_2_.5, bf16[512,1024]{1,0:T(8,128)(2,1)} %get-tuple-element.26.refs_3_, ...), custom_call_target="tpu_custom_call" | custom-call | tf_op jit(solution)/shard_map/keys/pallas_call | solution.py:469
  190.2 0.4 all-to-all-done.3.recv_ref
  190.6 0.0 copy-start.2
  190.6 1.3 copy-done.2
  191.9 4.3 %all-to-all-start.2 = ((bf16[8,1024,128]{2,1,0:T(8,128)(2,1)}), bf16[8,1024,128]{2,1,0:T(8,128)(2,1)}, u32[]{:S(2)}, u32[]{:S(2)}) async-start(bf16[8,1024,128]{2,1,0:T(8,128)(2,1)} %get-tuple-element.32), calls=%async_computation.2 | async-start | bytes 4194304 | tf_op jit(solution)/shard_map/all_to_all | solution.py:580
  196.3 4.3 %shard_map.90 = bf16[4096,256]{1,0:T(8,128)(2,1)} custom-call(s32[8,6]{1,0:T(8,128)} %sel_ref.7, s32[1]{0:T(128)} %bitcast.pos_ref.refs_1_, bf16[6,1024,128]{2,1,0:T(8,128)(2,1)} %get-tuple-element.33.local_ref, bf16[8,1024,128]{2,1,0:T(8,128)(2,1)} %copy-done.2), custom_call_target="tpu_custom_call" | custom-call | tf_op jit(solution)/shard_map/pallas_call | solution.py:543
  200.6 22.3 %all-to-all-done.2.recv_ref = bf16[8,1024,128]{2,1,0:T(8,128)(2,1)} async-done(((bf16[8,1024,128]{2,1,0:T(8,128)(2,1)}), bf16[8,1024,128]{2,1,0:T(8,128)(2,1)}, u32[]{:S(2)}, u32[]{:S(2)}) %all-to-all-start.2) | async-done | bytes 2097184 | tf_op jit(solution)/shard_map/all_to_all | solution.py:580
  222.9 4.3 %shard_map.89 = bf16[4096,256]{1,0:T(8,128)(2,1)} custom-call(s32[8,6]{1,0:T(8,128)} %sel_ref.7, s32[1]{0:T(128)} %bitcast.pos_ref.refs_1_, bf16[6,1024,128]{2,1,0:T(8,128)(2,1)} %get-tuple-element.31.local_ref, bf16[8,1024,128]{2,1,0:T(8,128)(2,1)} %all-to-all-done.2.recv_ref), custom_call_target="tpu_custom_call" | custom-call | tf_op jit(solution)/shard_map/pallas_call | solution.py:543
Async XLA Ops:
  3.9 31.2 %all-to-all-start.1 = ((bf16[8,1024,128]{2,1,0:T(8,128)(2,1)}), bf16[8,1024,128]{2,1,0:T(8,128)(2,1)S(1)}, u32[]{:S(2)}, u32[]{:S(2)}) async-start(bf16[8,1024,128]{2,1,0:T(8,128)(2,1)} %shard_map.86), calls=%async_computation.1 | async-start | bytes 4194304 | tf_op jit(solution)/shard_map/all_to_all | solution.py:580
  35.1 1.3 copy-start.1
  36.4 90.0 %all-to-all-start = ((bf16[8,1024,128]{2,1,0:T(8,128)(2,1)}), bf16[8,1024,128]{2,1,0:T(8,128)(2,1)S(1)}, u32[]{:S(2)}, u32[]{:S(2)}) async-start(bf16[8,1024,128]{2,1,0:T(8,128)(2,1)} %shard_map.85), calls=%async_computation | async-start | bytes 4194304 | tf_op jit(solution)/shard_map/all_to_all | solution.py:580
  41.3 62.1 %copy-start.3 = (bf16[256,1024]{1,0:T(8,128)(2,1)}, bf16[256,1024]{1,0:T(8,128)(2,1)S(1)}, u32[]{:S(2)}) copy-start(bf16[256,1024]{1,0:T(8,128)(2,1)S(1)} %get-tuple-element.35.refs_1_) | copy-start | bytes 1572868
  41.3 62.1 %copy-start.4 = (bf16[256,1024]{1,0:T(8,128)(2,1)}, bf16[256,1024]{1,0:T(8,128)(2,1)S(1)}, u32[]{:S(2)}) copy-start(bf16[256,1024]{1,0:T(8,128)(2,1)S(1)} %get-tuple-element.36.refs_0_) | copy-start | bytes 1572868
  41.3 16.2 %collective-permute-start = (bf16[256,1024]{1,0:T(8,128)(2,1)S(1)}, bf16[256,1024]{1,0:T(8,128)(2,1)S(1)}, u32[]{:S(2)}, u32[]{:S(2)}) collective-permute-start(bf16[256,1024]{1,0:T(8,128)(2,1)S(1)} %get-tuple-element.36.refs_0_), channel_id=1, source_target_pairs={{0,1},{1,2},{2,3},{4,5},{5,6},{6,7},{8,9},{9,10},{10,11},{12,13},{... | collective-permute-start | bytes 1572872 | tf_op jit(solution)/shard_map/ppermute | solution.py:576
  45.3 22.9 %collective-permute-start.1 = (bf16[256,1024]{1,0:T(8,128)(2,1)S(1)}, bf16[256,1024]{1,0:T(8,128)(2,1)S(1)}, u32[]{:S(2)}, u32[]{:S(2)}) collective-permute-start(bf16[256,1024]{1,0:T(8,128)(2,1)S(1)} %get-tuple-element.35.refs_1_), channel_id=1, source_target_pairs={{0,1},{1,2},{2,3},{4,5},{5,6},{6,7},{8,9},{9,10},{10,11},{12,13},{... | collective-permute-start | bytes 1572872 | tf_op jit(solution)/shard_map/ppermute | solution.py:576
  48.8 20.9 %collective-permute-start.2 = (bf16[256,1024]{1,0:T(8,128)(2,1)S(1)}, bf16[256,1024]{1,0:T(8,128)(2,1)S(1)}, u32[]{:S(2)}, u32[]{:S(2)}) collective-permute-start(bf16[256,1024]{1,0:T(8,128)(2,1)S(1)} %get-tuple-element.36.refs_0_), channel_id=1, source_target_pairs={{1,0},{2,1},{3,2},{5,4},{6,5},{7,6},{9,8},{10,9},{11,10},{13,12},{... | collective-permute-start | bytes 1572872 | tf_op jit(solution)/shard_map/ppermute | solution.py:577
  50.1 25.5 %collective-permute-start.3 = (bf16[256,1024]{1,0:T(8,128)(2,1)S(1)}, bf16[256,1024]{1,0:T(8,128)(2,1)S(1)}, u32[]{:S(2)}, u32[]{:S(2)}) collective-permute-start(bf16[256,1024]{1,0:T(8,128)(2,1)S(1)} %get-tuple-element.35.refs_1_), channel_id=1, source_target_pairs={{1,0},{2,1},{3,2},{5,4},{6,5},{7,6},{9,8},{10,9},{11,10},{13,12},{... | collective-permute-start | bytes 1572872 | tf_op jit(solution)/shard_map/ppermute | solution.py:577
  57.5 18.0 %copy-start.5 = (bf16[256,1024]{1,0:T(8,128)(2,1)}, bf16[256,1024]{1,0:T(8,128)(2,1)S(1)}, u32[]{:S(2)}) copy-start(bf16[256,1024]{1,0:T(8,128)(2,1)S(1)} %collective-permute-done.refs_2_) | copy-start | bytes 1572868
  57.5 19.3 %collective-permute-start.4 = (bf16[256,1024]{1,0:T(8,128)(2,1)S(1)}, bf16[256,1024]{1,0:T(8,128)(2,1)}, u32[]{:S(2)}, u32[]{:S(2)}) collective-permute-start(bf16[256,1024]{1,0:T(8,128)(2,1)S(1)} %collective-permute-done.refs_2_), channel_id=1, source_target_pairs={{1,2},{2,3},{5,6},{6,7},{9,10},{10,11},{13,14},{14,15},{17,18},{18... | collective-permute-start | bytes 1572872 | tf_op jit(solution)/shard_map/ppermute | solution.py:576
  68.2 8.7 %copy-start.6 = (bf16[256,1024]{1,0:T(8,128)(2,1)}, bf16[256,1024]{1,0:T(8,128)(2,1)S(1)}, u32[]{:S(2)}) copy-start(bf16[256,1024]{1,0:T(8,128)(2,1)S(1)} %collective-permute-done.1.refs_3_) | copy-start | bytes 1572868
  68.2 10.1 %collective-permute-start.5 = (bf16[256,1024]{1,0:T(8,128)(2,1)S(1)}, bf16[256,1024]{1,0:T(8,128)(2,1)}, u32[]{:S(2)}, u32[]{:S(2)}) collective-permute-start(bf16[256,1024]{1,0:T(8,128)(2,1)S(1)} %collective-permute-done.1.refs_3_), channel_id=1, source_target_pairs={{1,2},{2,3},{5,6},{6,7},{9,10},{10,11},{13,14},{14,15},{17,18},{18... | collective-permute-start | bytes 1572872 | tf_op jit(solution)/shard_map/ppermute | solution.py:576
  69.7 8.7 %copy-start.7 = (bf16[256,1024]{1,0:T(8,128)(2,1)}, bf16[256,1024]{1,0:T(8,128)(2,1)S(1)}, u32[]{:S(2)}) copy-start(bf16[256,1024]{1,0:T(8,128)(2,1)S(1)} %collective-permute-done.2.refs_4_) | copy-start | bytes 1572868
  69.7 20.6 %collective-permute-start.6 = (bf16[256,1024]{1,0:T(8,128)(2,1)S(1)}, bf16[256,1024]{1,0:T(8,128)(2,1)}, u32[]{:S(2)}, u32[]{:S(2)}) collective-permute-start(bf16[256,1024]{1,0:T(8,128)(2,1)S(1)} %collective-permute-done.2.refs_4_), channel_id=1, source_target_pairs={{1,0},{2,1},{5,4},{6,5},{9,8},{10,9},{13,12},{14,13},{17,16},{18,1... | collective-permute-start | bytes 1572872 | tf_op jit(solution)/shard_map/ppermute | solution.py:577
  75.6 14.7 %copy-start.8 = (bf16[256,1024]{1,0:T(8,128)(2,1)}, bf16[256,1024]{1,0:T(8,128)(2,1)S(1)}, u32[]{:S(2)}) copy-start(bf16[256,1024]{1,0:T(8,128)(2,1)S(1)} %collective-permute-done.3.refs_5_) | copy-start | bytes 1572868
  75.6 26.0 %collective-permute-start.7 = (bf16[256,1024]{1,0:T(8,128)(2,1)S(1)}, bf16[256,1024]{1,0:T(8,128)(2,1)}, u32[]{:S(2)}, u32[]{:S(2)}) collective-permute-start(bf16[256,1024]{1,0:T(8,128)(2,1)S(1)} %collective-permute-done.3.refs_5_), channel_id=1, source_target_pairs={{1,0},{2,1},{5,4},{6,5},{9,8},{10,9},{13,12},{14,13},{17,16},{18,1... | collective-permute-start | bytes 1572872 | tf_op jit(solution)/shard_map/ppermute | solution.py:577
  76.9 65.8 %collective-permute-start.10 = (bf16[256,1024]{1,0:T(8,128)(2,1)}, bf16[256,1024]{1,0:T(8,128)(2,1)}, u32[]{:S(2)}, u32[]{:S(2)}) collective-permute-start(bf16[256,1024]{1,0:T(8,128)(2,1)} %collective-permute-done.4.refs_6_), channel_id=1, source_target_pairs={{2,3},{6,7},{10,11},{14,15},{18,19},{22,23},{26,27},{30,31}} | collective-permute-start | bytes 1572872 | tf_op jit(solution)/shard_map/ppermute | solution.py:576
  78.4 64.4 %collective-permute-start.11 = (bf16[256,1024]{1,0:T(8,128)(2,1)}, bf16[256,1024]{1,0:T(8,128)(2,1)}, u32[]{:S(2)}, u32[]{:S(2)}) collective-permute-start(bf16[256,1024]{1,0:T(8,128)(2,1)} %collective-permute-done.5.refs_7_), channel_id=1, source_target_pairs={{2,3},{6,7},{10,11},{14,15},{18,19},{22,23},{26,27},{30,31}} | collective-permute-start | bytes 1572872 | tf_op jit(solution)/shard_map/ppermute | solution.py:576
  90.3 52.4 %collective-permute-start.8 = (bf16[256,1024]{1,0:T(8,128)(2,1)}, bf16[256,1024]{1,0:T(8,128)(2,1)}, u32[]{:S(2)}, u32[]{:S(2)}) collective-permute-start(bf16[256,1024]{1,0:T(8,128)(2,1)} %collective-permute-done.6.refs_8_), channel_id=1, source_target_pairs={{1,0},{5,4},{9,8},{13,12},{17,16},{21,20},{25,24},{29,28}} | collective-permute-start | bytes 1572872 | tf_op jit(solution)/shard_map/ppermute | solution.py:577
  101.5 41.2 %collective-permute-start.9 = (bf16[256,1024]{1,0:T(8,128)(2,1)}, bf16[256,1024]{1,0:T(8,128)(2,1)}, u32[]{:S(2)}, u32[]{:S(2)}) collective-permute-start(bf16[256,1024]{1,0:T(8,128)(2,1)} %collective-permute-done.7.refs_9_), channel_id=1, source_target_pairs={{1,0},{5,4},{9,8},{13,12},{17,16},{21,20},{25,24},{29,28}} | collective-permute-start | bytes 1572872 | tf_op jit(solution)/shard_map/ppermute | solution.py:577
  126.4 1.3 copy-start
  159.9 30.7 %all-to-all-start.3 = ((bf16[8,1024,128]{2,1,0:T(8,128)(2,1)}), bf16[8,1024,128]{2,1,0:T(8,128)(2,1)S(1)}, u32[]{:S(2)}, u32[]{:S(2)}) async-start(bf16[8,1024,128]{2,1,0:T(8,128)(2,1)} %get-tuple-element.34), calls=%async_computation.3 | async-start | bytes 4194304 | tf_op jit(solution)/shard_map/all_to_all | solution.py:580
  190.6 1.3 copy-start.2
  191.9 31.0 %all-to-all-start.2 = ((bf16[8,1024,128]{2,1,0:T(8,128)(2,1)}), bf16[8,1024,128]{2,1,0:T(8,128)(2,1)}, u32[]{:S(2)}, u32[]{:S(2)}) async-start(bf16[8,1024,128]{2,1,0:T(8,128)(2,1)} %get-tuple-element.32), calls=%async_computation.2 | async-start | bytes 4194304 | tf_op jit(solution)/shard_map/all_to_all | solution.py:580
